TPU v7x, 32 devices: a whole 2x2x4 slice. The times are simulated.
32 devices in a mesh: task: 2 (over x), batch: 16 (over z, y, core).
Axes of the slice: x: 2, y: 2, z: 4, core: 2. Of those that a mesh axis runs over, the one named last changes fastest.
Arguments:
- pooled: bfloat16 [12288, 3328], P('batch'), may hold values from -6 to 6
- gate_weight: bfloat16 [3328, 8, 4], P(None, 'task'), may hold values from -0.21875 to 0.21875
- w_first: bfloat16 [8, 3328, 1024], P('task', 'batch'), may hold values from -0.15625 to 0.15625
- w_second: bfloat16 [8, 1024, 512], P('task', 'batch'), may hold values from -0.25 to 0.25
- w_third: bfloat16 [8, 512, 256], P('task', 'batch'), may hold values from -0.375 to 0.375
- tower_hidden: bfloat16 [4, 256, 128], P('task'), may hold values from -0.5 to 0.5
- tower_out: bfloat16 [4, 128], P('task'), may hold values from -0.75 to 0.75
Outputs:
- task_logits: float32 [12288, 4], P('batch', 'task')
All inputs are finite; a program needn't handle non-finite values.
Results may differ from a plain program's by a relative error of at most 0.02.
Values may be sent and summed in bfloat16 or wider, within the bound.
A program may use at most 128 MiB of HBM per device.

v0:
```python
import jax
import jax.numpy as jnp
from jax import lax
from jax.sharding import PartitionSpec as P


def per_device(pooled, gate_weight, w_first, w_second, w_third, tower_hidden, tower_out):
    tok_rows = pooled.shape[0]
    width_in = pooled.shape[1]
    local_experts = w_first.shape[0]
    all_tasks = gate_weight.shape[2]
    own_tasks = tower_hidden.shape[0]
    gathered = lax.all_gather(w_first, "batch", axis=1, tiled=True)
    summed = jnp.einsum("tr,erh->eth", pooled, gathered, preferred_element_type=jnp.float32)
    first = jax.nn.relu(summed).astype(jnp.bfloat16)
    logits = jnp.dot(
        pooled,
        gate_weight.reshape(width_in, local_experts * all_tasks),
        preferred_element_type=jnp.float32,
    )
    weights = jnp.exp(logits.reshape(tok_rows, local_experts, all_tasks))
    gate_total = jnp.sum(weights, axis=1)
    columns = first
    second = jax.nn.relu(
        jnp.einsum(
            "etr,erh->eth",
            columns,
            lax.all_gather(w_second, "batch", axis=1, tiled=True),
            preferred_element_type=jnp.float32,
        )
    ).astype(jnp.bfloat16)
    columns = second
    expert_out = jax.nn.relu(
        jnp.einsum(
            "etr,erh->eth",
            columns,
            lax.all_gather(w_third, "batch", axis=1, tiled=True),
            preferred_element_type=jnp.float32,
        )
    ).astype(jnp.bfloat16)
    numer = jnp.einsum("tek,eth->tkh", weights, expert_out.astype(jnp.float32))
    numer_all, total_all = (
        lax.psum(numer.astype(jnp.bfloat16), "task").astype(jnp.float32),
        lax.psum(gate_total.astype(jnp.bfloat16), "task").astype(jnp.float32),
    )
    first_task = lax.axis_index("task") * own_tasks
    numer_own = lax.dynamic_slice_in_dim(numer_all, first_task, own_tasks, 1)
    total_own = lax.dynamic_slice_in_dim(total_all, first_task, own_tasks, 1)
    mix = (numer_own / total_own[:, :, None]).astype(jnp.bfloat16)
    tower = jax.nn.relu(
        jnp.einsum("tkh,khm->tkm", mix, tower_hidden, preferred_element_type=jnp.float32)
    ).astype(jnp.bfloat16)
    return jnp.einsum("tkm,km->tk", tower, tower_out, preferred_element_type=jnp.float32)


def solution(mesh):
    placed = (
        P("batch", None),
        P(None, "task", None),
        P("task", "batch", None),
        P("task", "batch", None),
        P("task", "batch", None),
        P("task", None, None),
        P("task", None),
    )
    return jax.shard_map(
        per_device, mesh=mesh, in_specs=placed, out_specs=P("batch", "task"), check_vma=False
    )
```

profile of v0, /device:TPU:0, one launch (start us, length us, event | category | flops | bytes accessed | tf_op | source)
XLA Modules:
  0.0 307.8 jit_solution(7706464251963237315)
XLA Ops:
  6.5 0.0 copy-start
  6.5 0.0 all-gather.6.cloned.1.call-start
  6.5 0.7 all-gather.6.cloned.1.call-update
  7.3 0.0 all-gather.4.cloned.1.call-start
  7.3 0.7 all-gather.4.cloned.1.call-update
  8.0 0.0 all-gather.8.cloned.1.call-start
  8.1 0.7 all-gather.8.cloned.1.call-update
  8.7 0.0 all-reduce.2.cloned.1.call-start
  8.8 0.9 reshape.6
  9.8 4.1 %fusion.27 = (bf16[768,4]{0,1:T(4,128)(2,1)S(1)}, bf16[768,4,4]{0,2,1:T(4,128)(2,1)S(1)}) fusion(bf16[4,4,3328]{2,1,0:T(4,128)(2,1)S(1)} %dot_general.26, bf16[768,3328]{1,0:T(8,128)(2,1)} %param.7), kind=kOutput, calls=%fused_computation.28 | convolution fusion | flops 81810432 | bytes 5249024 | tf_op jit(solution)/shard_map/dot_general | solution.py:16
  13.8 0.6 copy.9
  14.4 48.2 %all-gather.6.cloned.1.call-done = bf16[4,1024,512]{2,1,0:T(8,128)(2,1)} async-done(((bf16[4,64,512]{2,1,0:T(8,128)(2,1)}), bf16[4,1024,512]{2,1,0:T(8,128)(2,1)}) %all-gather.6.cloned.1.call-update) | async-done | bytes 4194320 | tf_op jit(solution)/shard_map/all_gather | solution.py:28
  62.7 138.5 %all-gather.4.cloned.1.call-done = bf16[4,3328,1024]{2,1,0:T(8,128)(2,1)} async-done(((bf16[4,208,1024]{2,1,0:T(8,128)(2,1)}), bf16[4,3328,1024]{2,1,0:T(8,128)(2,1)}) %all-gather.4.cloned.1.call-update) | async-done | bytes 27262992 | tf_op jit(solution)/shard_map/all_gather | solution.py:13
  201.2 36.5 %fusion = bf16[4,768,512]{2,1,0:T(8,128)(2,1)} fusion(bf16[4,1024,512]{2,1,0:T(8,128)(2,1)} %all-gather.6.cloned.1.call-done, bf16[4,3328,1024]{2,1,0:T(8,128)(2,1)} %all-gather.4.cloned.1.call-done, bf16[768,3328]{1,0:T(8,128)(2,1)} %param.7), kind=kOutput, calls=%fused_computation.1 | convolution fusion | flops 24165482496 | bytes 39714816 | tf_op jit(solution)/shard_map/etr,erh->eth/dot_general | solution.py:25
  237.7 3.5 %all-gather.8.cloned.1.call-done = bf16[4,512,256]{2,1,0:T(8,128)(2,1)} async-done(((bf16[4,32,256]{2,1,0:T(8,128)(2,1)}), bf16[4,512,256]{2,1,0:T(8,128)(2,1)}) %all-gather.8.cloned.1.call-update) | async-done | bytes 1048592 | tf_op jit(solution)/shard_map/all_gather | solution.py:37
  241.3 3.2 %maximum_convert_fusion.4 = bf16[4,768,256]{2,1,0:T(8,128)(2,1)S(1)} fusion(bf16[4,512,256]{2,1,0:T(8,128)(2,1)} %all-gather.8.cloned.1.call-done, bf16[4,768,512]{2,1,0:T(8,128)(2,1)} %fusion), kind=kOutput, calls=%fused_computation.9 | convolution fusion | flops 811597824 | bytes 5767168 | tf_op jit(solution)/shard_map/etr,erh->eth/dot_general | solution.py:34
  244.4 0.0 copy-start.1
  244.4 2.6 convolution_convert_fusion
  247.0 0.0 all-reduce.2.cloned.1.call-update
  247.0 5.0 %psum.15 = bf16[768,4]{0,1:T(4,128)(2,1)S(1)} all-reduce(bf16[768,4]{0,1:T(4,128)(2,1)S(1)} %get-tuple-element.5), channel_id=1, replica_groups=mesh['task'=2,'batch'=16] {'task'}, use_global_device_ids=true, to_apply=%region_2.3 | all-reduce | flops 3072 | bytes 12288 | tf_op jit(solution)/shard_map/psum | solution.py:44
  252.1 0.2 copy.8
  252.2 45.5 %all-reduce.2.cloned.1.call-done = bf16[768,4,256]{2,1,0:T(4,128)(2,1)} async-done(((bf16[768,4,256]{2,1,0:T(4,128)(2,1)}), bf16[768,4,256]{2,1,0:T(4,128)(2,1)}) %all-reduce.2.cloned.1.call-update) | async-done | bytes 1572880 | tf_op jit(solution)/shard_map/psum | solution.py:43
  297.7 2.5 fusion.13
  300.2 0.0 copy-done
  300.2 0.0 copy-done.1
  300.2 0.5 fusion.16
  300.7 0.6 copy.22
  (2 shorter events, 0.0 us)
Async XLA Ops:
  6.5 293.6 %copy-start = (bf16[2,256,128]{2,1,0:T(8,128)(2,1)S(1)}, bf16[2,256,128]{2,1,0:T(8,128)(2,1)}, u32[]{:S(2)}) copy-start(bf16[2,256,128]{2,1,0:T(8,128)(2,1)} %param.12) | copy-start | bytes 393220
  6.5 56.1 %all-gather.6.cloned.1.call-start = ((), (), s32[]{:S(2)}) async-start(), calls=%async_computation.1 | async-start | bytes 4456448 | tf_op jit(solution)/shard_map/all_gather | solution.py:28
  7.3 193.9 %all-gather.4.cloned.1.call-start = ((), (), s32[]{:S(2)}) async-start(), calls=%async_computation | async-start | bytes 28966912 | tf_op jit(solution)/shard_map/all_gather | solution.py:13
  8.0 233.3 %all-gather.8.cloned.1.call-start = ((), (), s32[]{:S(2)}) async-start(), calls=%async_computation.2 | async-start | bytes 1114112 | tf_op jit(solution)/shard_map/all_gather | solution.py:37
  8.7 289.0 %all-reduce.2.cloned.1.call-start = ((), (), s32[]{:S(2)}) async-start(), calls=%async_computation.3 | async-start | bytes 3145728 | tf_op jit(solution)/shard_map/psum | solution.py:43
  244.4 55.8 %copy-start.1 = (bf16[2,128]{1,0:T(2,128)(2,1)S(1)}, bf16[2,128]{1,0:T(2,128)(2,1)}, u32[]{:S(2)}) copy-start(bf16[2,128]{1,0:T(2,128)(2,1)} %param.13) | copy-start | bytes 1540
Sparse Core Ops, SparseCore 0:
  9.5 53.1 all-gather.5
  64.2 136.9 all-gather.3
  203.4 37.8 all-gather.7
  247.2 50.5 all-reduce.1
where the time goes:
time: 308 us
  waiting for transfers between devices  238 us (77%)
  matrix products  46.8 us (15%)
  between operations  13.2 us (4%)
  blocking collectives  5 us (2%)
    all_gather x1, waiting for transfers between devices, per_device(): gathered = lax.all_gather(w_first, 'batch', axis=1, tiled=True)  139 us
    all_gather x1, waiting for transfers between devices, per_device(): lax.all_gather(w_second, 'batch', axis=1, tiled=True)  48.2 us
    psum x1, waiting for transfers between devices, per_device(): lax.psum(numer.astype(jnp.bfloat16), 'task').astype(jnp.float32)  45.5 us
    dot_general x1, matrix products, per_device(): jnp.einsum('etr,erh->eth', columns, lax.all_gather(w_second, 'batch', axi...  36.5 us
  transfers between devices with their start and end apart: 4, of which 4 were waited for; matrix products, arithmetic and copies ran while one was open for 14% of the time, Pallas kernels for 0%

commit v1 on v0

--- a/solution.py
+++ b/solution.py
@@ -11,6 +11,19 @@
     all_tasks = gate_weight.shape[2]
     own_tasks = tower_hidden.shape[0]
     gathered = lax.all_gather(w_first, "batch", axis=1, tiled=True)
+    deep_rows, deep_width = w_second.shape[1], w_second.shape[2]
+    last_rows, last_width = w_third.shape[1], w_third.shape[2]
+    halves = deep_width // last_width
+    packed = jnp.concatenate(
+        [w_second[:, :, i * last_width : (i + 1) * last_width] for i in range(halves)] + [w_third],
+        axis=1,
+    )
+    gathered, packed = lax.optimization_barrier((gathered, packed))
+    packed = lax.all_gather(packed, "batch", axis=1, tiled=False)
+    second_all = jnp.concatenate(
+        [packed[:, :, i * deep_rows : (i + 1) * deep_rows] for i in range(halves)], axis=3
+    ).reshape(local_experts, -1, deep_width)
+    third_all = packed[:, :, halves * deep_rows :].reshape(local_experts, -1, last_width)
     summed = jnp.einsum("tr,erh->eth", pooled, gathered, preferred_element_type=jnp.float32)
     first = jax.nn.relu(summed).astype(jnp.bfloat16)
     logits = jnp.dot(
@@ -25,7 +38,7 @@
         jnp.einsum(
             "etr,erh->eth",
             columns,
-            lax.all_gather(w_second, "batch", axis=1, tiled=True),
+            second_all,
             preferred_element_type=jnp.float32,
         )
     ).astype(jnp.bfloat16)
@@ -34,18 +47,22 @@
         jnp.einsum(
             "etr,erh->eth",
             columns,
-            lax.all_gather(w_third, "batch", axis=1, tiled=True),
+            third_all,
             preferred_element_type=jnp.float32,
         )
     ).astype(jnp.bfloat16)
     numer = jnp.einsum("tek,eth->tkh", weights, expert_out.astype(jnp.float32))
-    numer_all, total_all = (
-        lax.psum(numer.astype(jnp.bfloat16), "task").astype(jnp.float32),
-        lax.psum(gate_total.astype(jnp.bfloat16), "task").astype(jnp.float32),
-    )
-    first_task = lax.axis_index("task") * own_tasks
-    numer_own = lax.dynamic_slice_in_dim(numer_all, first_task, own_tasks, 1)
-    total_own = lax.dynamic_slice_in_dim(total_all, first_task, own_tasks, 1)
+    groups = all_tasks // own_tasks
+    me = lax.axis_index("task")
+    numer_own = lax.dynamic_slice_in_dim(numer, me * own_tasks, own_tasks, 1)
+    total_own = lax.dynamic_slice_in_dim(gate_total, me * own_tasks, own_tasks, 1)
+    for shift in range(1, groups):
+        ring = [(i, (i + shift) % groups) for i in range(groups)]
+        other = lax.rem(me + shift, groups) * own_tasks
+        numer_sent = lax.dynamic_slice_in_dim(numer, other, own_tasks, 1).astype(jnp.bfloat16)
+        total_sent = lax.dynamic_slice_in_dim(gate_total, other, own_tasks, 1)
+        numer_own = numer_own + lax.ppermute(numer_sent, "task", ring).astype(jnp.float32)
+        total_own = total_own + lax.ppermute(total_sent, "task", ring)
     mix = (numer_own / total_own[:, :, None]).astype(jnp.bfloat16)
     tower = jax.nn.relu(
         jnp.einsum("tkh,khm->tkm", mix, tower_hidden, preferred_element_type=jnp.float32)

time: 308 us -> 291 us (0.945)
  waiting for transfers between devices: 238 us -> 211 us
  local copies, waits for them, and re-layouts: 2.39 us -> 10.6 us
  blocking collectives: 5 us -> 0 us
  other arithmetic: 2.47 us -> 7.28 us
    psum x1 -> x0, waiting for transfers between devices: 45.5 us -> none  [per_device(): lax.psum(numer.astype(jnp.bfloat16), 'task').astype(jnp.float32)]
    ppermute x0 -> x2, waiting for transfers between devices: none -> 18 us  [the longest x1 18 us: per_device(): total_own = total_own + lax.ppermute(total_sent, 'task', ring)]
    slice x0 -> x3, local copies, waits for them, and re-layouts: none -> 5.1 us  [the longest x1 2.81 us: per_device(): packed[:, :, i * deep_rows:(i + 1) * deep_rows]]
    psum x1 -> x0, blocking collectives: 5 us -> none  [per_device(): lax.psum(gate_total.astype(jnp.bfloat16), 'task').astype(jnp.float32)]
    concatenate x0 -> x2, other arithmetic: none -> 4.05 us  [the longest x1 2.46 us: per_device(): jnp.concatenate([packed[:, :, i * deep_rows:(i + 1) * deep_rows] for i in...]
    all_gather x2 -> x1, waiting for transfers between devices: 51.8 us -> 51.7 us  [per_device(): packed = lax.all_gather(packed, 'batch', axis=1, tiled=False)]
  transfers between devices with their start and end apart: 4 -> 4, of which waited for: 4 -> 3; matrix products, arithmetic and copies ran while one was open for 14% -> 3% of each run, Pallas kernels for 0% -> 0%
where the time goes in v1:
time: 291 us
  waiting for transfers between devices  211 us (73%)
  matrix products  46.7 us (16%)
  between operations  13.5 us (5%)
  local copies, waits for them, and re-layouts  10.6 us (4%)
  other arithmetic  7.28 us (3%)
    all_gather x1, waiting for transfers between devices, per_device(): gathered = lax.all_gather(w_first, 'batch', axis=1, tiled=True)  140 us
    all_gather x1, waiting for transfers between devices, per_device(): packed = lax.all_gather(packed, 'batch', axis=1, tiled=False)  51.7 us
    dot_general x1, matrix products, per_device(): jnp.einsum('etr,erh->eth', columns, second_all, preferred_element_type=jn...  36.6 us
    ppermute x1, waiting for transfers between devices, per_device(): total_own = total_own + lax.ppermute(total_sent, 'task', ring)  18 us
  transfers between devices with their start and end apart: 4, of which 3 were waited for; matrix products, arithmetic and copies ran while one was open for 3% of the time, Pallas kernels for 0%

profile of v1, /device:TPU:0, one launch (start us, length us, event | category | flops | bytes accessed | tf_op | source)
XLA Modules:
  0.0 290.8 jit_solution(5870801982256246528)
XLA Ops:
  6.5 0.0 copy-start
  6.5 0.0 all-gather.4.cloned.1.call-start
  6.5 0.7 all-gather.4.cloned.1.call-update
  7.3 0.0 all-gather.6.cloned.1.call-start
  7.3 1.0 fusion.32
  8.3 1.6 pad_maximum_fusion.1
  9.9 140.2 %all-gather.4.cloned.1.call-done = bf16[4,3328,1024]{2,1,0:T(8,128)(2,1)} async-done(((bf16[4,208,1024]{2,1,0:T(8,128)(2,1)}), bf16[4,3328,1024]{2,1,0:T(8,128)(2,1)}) %all-gather.4.cloned.1.call-update) | async-done | bytes 27262992 | tf_op jit(solution)/shard_map/all_gather | solution.py:13
  150.1 0.0 all-gather.6.cloned.1.call-update
  150.1 0.9 reshape.12
  151.0 4.1 %fusion.33 = (f32[768,4]{0,1:T(4,128)S(1)}, bf16[768,4,4]{0,2,1:T(4,128)(2,1)S(1)}) fusion(bf16[4,4,3328]{2,1,0:T(4,128)(2,1)S(1)} %dot_general.26, bf16[768,3328]{1,0:T(8,128)(2,1)} %param.7), kind=kOutput, calls=%fused_computation.36 | convolution fusion | flops 81810432 | bytes 5255168 | tf_op jit(solution)/shard_map/dot_general | solution.py:29
  155.1 1.3 copy.9
  156.4 51.7 %all-gather.6.cloned.1.call-done = bf16[4,2560,256]{2,1,0:T(8,128)(2,1)} async-done(((bf16[4,160,256]{2,1,0:T(8,128)(2,1)}), bf16[4,2560,256]{2,1,0:T(8,128)(2,1)}) %all-gather.6.cloned.1.call-update) | async-done | bytes 5242896 | tf_op jit(solution)/shard_map/all_gather | solution.py:22
  208.1 1.3 slice.22
  209.4 2.8 fusion.31
  212.2 2.5 pad_maximum_fusion
  214.7 36.6 %fusion = bf16[4,768,512]{2,1,0:T(8,128)(2,1)} fusion(bf16[4,1024,512]{2,1,0:T(8,128)(2,1)} %bitcast.37, bf16[4,3328,1024]{2,1,0:T(8,128)(2,1)} %all-gather.4.cloned.1.call-done, bf16[768,3328]{1,0:T(8,128)(2,1)} %param.7), kind=kOutput, calls=%fused_computation.1 | convolution fusion | flops 24165482496 | bytes 39714816 | tf_op jit(solution)/shard_map/etr,erh->eth/dot_general | solution.py:38
  251.3 0.0 copy-start.1
  251.3 2.9 %fusion.10 = bf16[4,768,256]{2,1,0:T(8,128)(2,1)S(1)} fusion(bf16[4,512,256]{2,1,0:T(8,128)(2,1)S(1)} %bitcast.38, bf16[4,768,512]{2,1,0:T(8,128)(2,1)} %fusion), kind=kOutput, calls=%fused_computation.9 | convolution fusion | flops 810024960 | bytes 5767168 | tf_op jit(solution)/shard_map/etr,erh->eth/dot_general | solution.py:47
  254.2 0.0 copy-done.1
  254.2 1.5 fusion.13
  255.8 0.0 copy-start.2
  255.8 1.6 dynamic-slice_convert_fusion
  257.4 1.5 collective-permute-start
  258.9 0.6 collective-permute-start.1
  259.4 18.0 %collective-permute-done.1 = f32[768,2]{0,1:T(2,128)S(1)} collective-permute-done((f32[768,2]{0,1:T(2,128)S(1)}, f32[768,2]{0,1:T(2,128)S(1)}, u32[]{:S(2)}, u32[]{:S(2)}) %collective-permute-start.1) | collective-permute-done | bytes 6176 | tf_op jit(solution)/shard_map/ppermute | solution.py:65
  277.5 0.9 copy.10
  278.4 0.0 collective-permute-done
  278.4 3.2 %fusion.16 = bf16[768,2,256]{2,1,0:T(2,128)(2,1)} fusion(bf16[768,2,256]{2,1,0:T(2,128)(2,1)} %collective-permute-done, f32[768,4,256]{2,1,0:T(4,128)S(1)} %fusion.13, s32[]{:T(128)S(6)} %select_n.8, f32[768,2]{1,0:T(8,128)} %copy.10), kind=kLoop, calls=%fused_computation.17 | loop fusion | flops 1572864 | bytes 3151876 | tf_op jit(solution)/shard_map/convert_element_type | solution.py:66
  281.7 0.0 copy-done
  281.7 0.0 copy-done.2
  281.7 1.6 fusion.19
  283.3 0.6 copy.25
  (3 shorter events, 0.0 us)
Async XLA Ops:
  6.5 275.1 %copy-start = (bf16[2,256,128]{2,1,0:T(8,128)(2,1)S(1)}, bf16[2,256,128]{2,1,0:T(8,128)(2,1)}, u32[]{:S(2)}) copy-start(bf16[2,256,128]{2,1,0:T(8,128)(2,1)} %param.12) | copy-start | bytes 393220
  6.5 143.5 %all-gather.4.cloned.1.call-start = ((), (), s32[]{:S(2)}) async-start(), calls=%async_computation | async-start | bytes 28966912 | tf_op jit(solution)/shard_map/all_gather | solution.py:13
  7.3 200.9 %all-gather.6.cloned.1.call-start = ((), (), s32[]{:S(2)}) async-start(), calls=%async_computation.1 | async-start | bytes 5570560 | tf_op jit(solution)/shard_map/all_gather | solution.py:22
  251.3 3.0 %copy-start.1 = (bf16[768,4,4]{1,2,0:T(4,128)(2,1)S(1)}, bf16[768,4,4]{1,2,0:T(4,128)(2,1)}, u32[]{:S(2)}) copy-start(bf16[768,4,4]{1,2,0:T(4,128)(2,1)} %copy.9) | copy-start | bytes 73732
  255.8 25.9 %copy-start.2 = (bf16[2,128]{1,0:T(2,128)(2,1)S(1)}, bf16[2,128]{1,0:T(2,128)(2,1)}, u32[]{:S(2)}) copy-start(bf16[2,128]{1,0:T(2,128)(2,1)} %param.13) | copy-start | bytes 1540
  257.4 21.0 %collective-permute-start = (bf16[768,2,256]{2,1,0:T(2,128)(2,1)}, bf16[768,2,256]{2,1,0:T(2,128)(2,1)}, u32[]{:S(2)}, u32[]{:S(2)}) collective-permute-start(bf16[768,2,256]{2,1,0:T(2,128)(2,1)} %dynamic-slice_convert_fusion), channel_id=1, source_target_pairs={{0,16},{16,0},{1,17},{17,1},{2,18},{18,2},{3,19},{19,3},{4,20},{20... | collective-permute-start | bytes 2359304 | tf_op jit(solution)/shard_map/ppermute | solution.py:64
  258.9 18.6 %collective-permute-start.1 = (f32[768,2]{0,1:T(2,128)S(1)}, f32[768,2]{0,1:T(2,128)S(1)}, u32[]{:S(2)}, u32[]{:S(2)}) collective-permute-start(f32[768,2]{0,1:T(2,128)S(1)} %constant_dynamic-slice_fusion), channel_id=1, source_target_pairs={{0,16},{16,0},{1,17},{17,1},{2,18},{18,2},{3,19},{19,3},{4,20},{20... | collective-permute-start | bytes 18440 | tf_op jit(solution)/shard_map/ppermute | solution.py:65
Sparse Core Ops, SparseCore 0:
  8.9 141.1 all-gather.3
  152.3 55.7 all-gather.5

commit v2 on v1

--- a/solution.py
+++ b/solution.py
@@ -1,10 +1,375 @@
+import functools
+
 import jax
 import jax.numpy as jnp
 from jax import lax
+from jax.experimental import pallas as pl
+from jax.experimental.pallas import tpu as pltpu
 from jax.sharding import PartitionSpec as P
 
-
-def per_device(pooled, gate_weight, w_first, w_second, w_third, tower_hidden, tower_out):
+MESH = pl.DeviceIdType.MESH
+BF16, F32 = jnp.bfloat16, jnp.float32
+VMEM_BYTES = 63 * 1024 * 1024
+
+
+def dot(a, b):
+    return jnp.dot(a, b, preferred_element_type=F32)
+
+
+def fused_kernel(
+    nb, tiles, deep_rows,
+    pooled, gate, w_first, packed, tower_hidden, tower_out, out,
+    buf, dbuf, first, outs, outs_rx, wts, wts_rx, acc,
+    loc, recv, szp, szm, sy, ssib, brecv, bzp, bzm, by, bsib, xs, xr, ws, wr,
+):
+    t, b = lax.axis_index("task"), lax.axis_index("batch")
+    nz = nb // 4
+    z, y, c = b // 4, (b // 2) % 2, b % 2
+    experts = outs.shape[0]
+    tasks = tower_hidden.shape[0]
+    chunks = buf.shape[0]
+    wide = buf.shape[3]
+    tile = pooled.shape[0] // tiles
+
+    def at(zz, yy, cc):
+        return zz * 4 + yy * 2 + cc
+
+    across, sib = at(z, 1 - y, c), at(z, y, 1 - c)
+    up, down = at(z + 1, y, c), at(z - 1, y, c)
+
+    def own_copy(k):
+        return pltpu.make_async_copy(
+            w_first.at[k // 2, :, pl.ds(pl.multiple_of((k % 2) * wide, 128), wide)],
+            buf.at[k, b], loc.at[k],
+        )
+
+    deep_copy = pltpu.make_async_copy(packed, dbuf.at[b], loc.at[chunks])
+    deep_copy.start()
+
+    @pl.loop(0, chunks)
+    def _(k):
+        own_copy(k).start()
+
+    barrier = pltpu.get_barrier_semaphore()
+    for peer in (across, sib, at((z + 1) % nz, y, c), at((z + nz - 1) % nz, y, c)):
+        pl.semaphore_signal(barrier, inc=1, device_id=(t, peer), device_id_type=MESH)
+    pl.semaphore_signal(barrier, inc=1, device_id=(1 - t, b), device_id_type=MESH)
+    pl.semaphore_wait(barrier, 5)
+
+    def move(k, slot, sem, dev):
+        return pltpu.make_async_remote_copy(
+            src_ref=buf.at[k, slot], dst_ref=buf.at[k, slot], send_sem=sem,
+            recv_sem=recv.at[k, slot], device_id=(t, dev), device_id_type=MESH,
+        )
+
+    def bmove(slot, sem, dev):
+        return pltpu.make_async_remote_copy(
+            src_ref=dbuf.at[slot], dst_ref=dbuf.at[slot], send_sem=sem,
+            recv_sem=brecv.at[slot], device_id=(t, dev), device_id_type=MESH,
+        )
+
+    def arrived(k, slot):
+        move(k, slot, sy.at[0, 0], sib).wait_recv()
+
+    def barrived(slot):
+        bmove(slot, by.at[0], sib).wait_recv()
+
+    def own_z(k):
+        @pl.when(z < nz - 1)
+        def _():
+            move(k, b, szp.at[k, z], up).start()
+
+        @pl.when(z > 0)
+        def _():
+            move(k, b, szm.at[k, z], down).start()
+
+    def z_step(k, d):
+        @pl.when(z >= d)
+        def _():
+            slot = at(z - d, y, c)
+            arrived(k, slot)
+
+            @pl.when(z < nz - 1)
+            def _():
+                move(k, slot, szp.at[k, z - d], up).start()
+
+            move(k, slot, sy.at[k, z - d], across).start()
+            move(k, slot, ssib.at[k, z - d], sib).start()
+
+        @pl.when(z + d < nz)
+        def _():
+            slot = at(z + d, y, c)
+            arrived(k, slot)
+
+            @pl.when(z > 0)
+            def _():
+                move(k, slot, szm.at[k, z + d], down).start()
+
+            move(k, slot, sy.at[k, z + d], across).start()
+            move(k, slot, ssib.at[k, z + d], sib).start()
+
+    def y_step(k):
+        @pl.loop(0, nz)
+        def _(zz):
+            slot = at(zz, 1 - y, c)
+            arrived(k, slot)
+            move(k, slot, ssib.at[k, nz + zz], sib).start()
+
+    def sib_wait(k):
+        @pl.loop(0, nz * 2)
+        def _(q):
+            arrived(k, q * 2 + (1 - c))
+
+    def b_send_z(slot, yy, zz):
+        @pl.when(jnp.logical_and(z < nz - 1, zz <= z))
+        def _():
+            bmove(slot, bzp.at[yy, zz], up).start()
+
+        @pl.when(jnp.logical_and(z > 0, zz >= z))
+        def _():
+            bmove(slot, bzm.at[yy, zz], down).start()
+
+    deep_copy.wait()
+    bmove(b, by.at[0], across).start()
+    b_send_z(b, y, z)
+    bmove(b, bsib.at[y, z], sib).start()
+
+    @pl.loop(0, chunks)
+    def _(k):
+        own_copy(k).wait()
+        move(k, b, sy.at[k, z], across).start()
+        move(k, b, ssib.at[k, z], sib).start()
+
+    barrived(across)
+    b_send_z(across, 1 - y, z)
+    bmove(across, bsib.at[1 - y, z], sib).start()
+    own_z(0)
+
+    for m in range(tiles):
+        rows = pl.ds(m * tile, tile)
+        wts[rows, :] = jnp.exp(dot(pooled[rows, :], gate[...]))
+    w_move = pltpu.make_async_remote_copy(
+        src_ref=wts, dst_ref=wts_rx, send_sem=ws.at[0], recv_sem=wr.at[0],
+        device_id=(1 - t, b), device_id_type=MESH,
+    )
+    w_move.start()
+    acc[...] = jnp.zeros_like(acc)
+
+    for d in range(1, nz):
+        for same in (True, False):
+            yy = y if same else 1 - y
+
+            @pl.when(z >= d)
+            def _():
+                slot = at(z - d, yy, c)
+                barrived(slot)
+                b_send_z(slot, yy, z - d)
+                bmove(slot, bsib.at[yy, z - d], sib).start()
+
+            @pl.when(z + d < nz)
+            def _():
+                slot = at(z + d, yy, c)
+                barrived(slot)
+                b_send_z(slot, yy, z + d)
+                bmove(slot, bsib.at[yy, z + d], sib).start()
+
+    @pl.loop(0, nz * 2)
+    def _(q):
+        barrived(q * 2 + (1 - c))
+
+    w_move.wait_recv()
+
+    def x_move(e, m):
+        rows = pl.ds(m * tile, tile)
+        return pltpu.make_async_remote_copy(
+            src_ref=outs.at[e, rows], dst_ref=outs_rx.at[e, rows],
+            send_sem=xs.at[e, m], recv_sem=xr.at[e, m],
+            device_id=(1 - t, b), device_id_type=MESH,
+        )
+
+    def accumulate(w_ref, base, e, m, value):
+        rows = pl.ds(m * tile, tile)
+        w = w_ref[rows, :]
+        lane = lax.broadcasted_iota(jnp.int32, w.shape, 1)
+        value = value.astype(F32)
+        for j in range(tasks):
+            column = jnp.sum(
+                jnp.where(lane == base + j * experts + e, w, 0.0), axis=1, keepdims=True
+            )
+            acc[j, rows, :] = acc[j, rows, :] + column * value
+
+    def compute(k, m):
+        rows = pl.ds(m * tile, tile)
+        weights = buf[k].reshape(-1, wide)
+        first[k % 2, rows, :] = jnp.maximum(dot(pooled[rows, :], weights), 0.0).astype(BF16)
+
+        @pl.when(k % 2 == 1)
+        def _():
+            e = k // 2
+            width = dbuf.shape[3]
+            low, high = first[0, rows, :], first[1, rows, :]
+            total = None
+            pieces = (dbuf.shape[2] - 1) // deep_rows
+            for h in range(pieces):
+                w2 = dbuf[:, e, pl.ds(h * deep_rows, deep_rows), :].reshape(-1, width)
+                second = dot(low, w2[:wide]) + dot(high, w2[wide:])
+                second = jnp.maximum(second, 0.0).astype(BF16)
+                w3 = dbuf[:, e, pl.ds(pieces * deep_rows, dbuf.shape[2] - pieces * deep_rows), :]
+                w3 = w3.reshape(-1, width)[h * width : (h + 1) * width]
+                part = dot(second, w3)
+                total = part if total is None else total + part
+            value = jnp.maximum(total, 0.0).astype(BF16)
+            outs[e, rows, :] = value
+            x_move(e, m).start()
+            accumulate(wts, 0, e, m, value)
+
+            @pl.when(e >= 1)
+            def _():
+                x_move(e - 1, m).wait_recv()
+                accumulate(wts_rx, tasks * experts, e - 1, m, outs_rx[e - 1, rows, :])
+
+    @pl.loop(0, chunks + 2)
+    def _(i):
+        @pl.when(i + 1 < chunks)
+        def _():
+            own_z(i + 1)
+
+        @pl.when(i >= 2)
+        def _():
+            sib_wait(i - 2)
+
+        for s in range(max(tiles, nz - 1)):
+            if s < tiles:
+                @pl.when(i >= 2)
+                def _():
+                    compute(i - 2, s)
+            if s + 1 < nz:
+                @pl.when(i < chunks)
+                def _():
+                    z_step(i, s + 1)
+
+        @pl.when(jnp.logical_and(i >= 1, i <= chunks))
+        def _():
+            y_step(i - 1)
+
+    for m in range(tiles):
+        rows = pl.ds(m * tile, tile)
+        x_move(experts - 1, m).wait_recv()
+        accumulate(wts_rx, tasks * experts, experts - 1, m, outs_rx[experts - 1, rows, :])
+        own, other = wts[rows, :], wts_rx[rows, :]
+        lane = lax.broadcasted_iota(jnp.int32, own.shape, 1)
+        for j in range(tasks):
+            lo = j * experts
+            hi = lo + tasks * experts
+            mine = jnp.logical_and(lane >= lo, lane < lo + experts)
+            theirs = jnp.logical_and(lane >= hi, lane < hi + experts)
+            total = jnp.sum(
+                jnp.where(mine, own, 0.0) + jnp.where(theirs, other, 0.0), axis=1, keepdims=True
+            )
+            mix = (acc[j, rows, :] / total).astype(BF16)
+            tower = jnp.maximum(dot(mix, tower_hidden[j]), 0.0).astype(BF16).astype(F32)
+            out[rows, j : j + 1] = jnp.sum(
+                tower * tower_out[j : j + 1, :].astype(F32), axis=1, keepdims=True
+            )
+
+    w_move.wait_send()
+    for m in range(tiles):
+        @pl.loop(0, experts)
+        def _(e):
+            x_move(e, m).wait_send()
+
+    bmove(b, by.at[0], across).wait_send()
+
+    @pl.loop(0, nz)
+    def _(zz):
+        for yy in range(2):
+            slot = at(zz, yy, c)
+            bmove(slot, bsib.at[yy, zz], sib).wait_send()
+
+            @pl.when(jnp.logical_and(z < nz - 1, zz <= z))
+            def _():
+                bmove(slot, bzp.at[yy, zz], up).wait_send()
+
+            @pl.when(jnp.logical_and(z > 0, zz >= z))
+            def _():
+                bmove(slot, bzm.at[yy, zz], down).wait_send()
+
+        slot = at(zz, y, c)
+
+        @pl.loop(0, chunks)
+        def _(k):
+            move(k, slot, sy.at[k, zz], across).wait_send()
+            move(k, slot, ssib.at[k, zz], sib).wait_send()
+            move(k, slot, ssib.at[k, nz + zz], sib).wait_send()
+
+            @pl.when(jnp.logical_and(z < nz - 1, zz <= z))
+            def _():
+                move(k, slot, szp.at[k, zz], up).wait_send()
+
+            @pl.when(jnp.logical_and(z > 0, zz >= z))
+            def _():
+                move(k, slot, szm.at[k, zz], down).wait_send()
+
+
+def fused(nb, pooled, gate_weight, w_first, w_second, w_third, tower_hidden, tower_out):
+    tokens, width_in = pooled.shape
+    experts, rows, h1 = w_first.shape
+    tasks = tower_hidden.shape[0]
+    all_tasks = gate_weight.shape[2]
+    deep_rows, deep_width = w_second.shape[1:]
+    last_rows, last_width = w_third.shape[1:]
+    nz = nb // 4
+    chunks, wide = experts * 2, h1 // 2
+    tiles = 3 if tokens % (3 * 16) == 0 else 1
+    me = lax.axis_index("task")
+    gate = jnp.roll(gate_weight, -me * tasks, axis=2)
+    gate = jnp.transpose(gate, (0, 2, 1)).reshape(width_in, all_tasks * experts)
+    gate = jnp.pad(gate, ((0, 0), (0, 128 - all_tasks * experts)))
+    packed = jnp.concatenate(
+        [w_second[:, :, i : i + last_width] for i in range(0, deep_width, last_width)]
+        + [w_third],
+        axis=1,
+    )
+    dma = pltpu.SemaphoreType.DMA
+    vmem = pl.BlockSpec(memory_space=pltpu.VMEM)
+    anywhere = pl.BlockSpec(memory_space=pl.ANY)
+    return pl.pallas_call(
+        functools.partial(fused_kernel, nb, tiles, deep_rows),
+        out_shape=jax.ShapeDtypeStruct((tokens, tasks), F32),
+        in_specs=[vmem, vmem, anywhere, anywhere, vmem, vmem],
+        out_specs=vmem,
+        scratch_shapes=[
+            pltpu.VMEM((chunks, nb, rows, wide), BF16),
+            pltpu.VMEM((nb,) + packed.shape, BF16),
+            pltpu.VMEM((2, tokens, wide), BF16),
+            pltpu.VMEM((experts, tokens, last_width), BF16),
+            pltpu.VMEM((experts, tokens, last_width), BF16),
+            pltpu.VMEM((tokens, 128), F32),
+            pltpu.VMEM((tokens, 128), F32),
+            pltpu.VMEM((tasks, tokens, last_width), F32),
+            dma((chunks + 1,)),
+            dma((chunks, nb)),
+            dma((chunks, nz)),
+            dma((chunks, nz)),
+            dma((chunks, nz)),
+            dma((chunks, 2 * nz)),
+            dma((nb,)),
+            dma((2, nz)),
+            dma((2, nz)),
+            dma((1,)),
+            dma((2, nz)),
+            dma((experts, tiles)),
+            dma((experts, tiles)),
+            dma((1,)),
+            dma((1,)),
+        ],
+        compiler_params=pltpu.CompilerParams(
+            collective_id=0, has_side_effects=True, vmem_limit_bytes=VMEM_BYTES
+        ),
+    )(pooled, gate, w_first, packed, tower_hidden, tower_out)
+
+
+def gathered_first(pooled, gate_weight, w_first, w_second, w_third, tower_hidden, tower_out):
     tok_rows = pooled.shape[0]
     width_in = pooled.shape[1]
     local_experts = w_first.shape[0]
@@ -70,6 +435,12 @@
     return jnp.einsum("tkm,km->tk", tower, tower_out, preferred_element_type=jnp.float32)
 
 
+def fits(mesh, pooled, gate_weight, w_first, w_second, w_third):
+    even = all(w.shape[1] % 16 == 0 for w in (w_first, w_second, w_third))
+    lanes = gate_weight.shape[1] * gate_weight.shape[2] <= 128
+    return even and lanes and mesh.shape["task"] == 2 and mesh.shape["batch"] % 4 == 0
+
+
 def solution(mesh):
     placed = (
         P("batch", None),
@@ -80,6 +451,12 @@
         P("task", None, None),
         P("task", None),
     )
+
+    def per_device(*args):
+        if fits(mesh, *args[:5]):
+            return fused(mesh.shape["batch"], *args)
+        return gathered_first(*args)
+
     return jax.shard_map(
         per_device, mesh=mesh, in_specs=placed, out_specs=P("batch", "task"), check_vma=False
     )

time: 291 us -> 197 us (0.68)
  waiting for transfers between devices: 211 us -> 0 us
  Pallas kernels: 0 us -> 190 us
  matrix products: 46.7 us -> 0 us
  between operations: 13.5 us -> 0.03 us
  local copies, waits for them, and re-layouts: 10.6 us -> 4.29 us
  other arithmetic: 7.28 us -> 2.78 us
    all_gather x2 -> x0, waiting for transfers between devices: 192 us -> none  [the longest x1 140 us: per_device(): gathered = lax.all_gather(w_first, 'batch', axis=1, tiled=True)]
    pallas_call x0 -> x1, Pallas kernels: none -> 190 us  [fused(): pl.pallas_call(functools.partial(fused_kernel, nb, tiles, deep_rows), out...]
    dot_general x5 -> x0, matrix products: 46.7 us -> none  [the longest x1 36.6 us: per_device(): jnp.einsum('etr,erh->eth', columns, second_all, preferred_element_type=jn...]
    ppermute x2 -> x0, waiting for transfers between devices: 18 us -> none  [the longest x1 18 us: per_device(): total_own = total_own + lax.ppermute(total_sent, 'task', ring)]
    slice x3 -> x1, local copies, waits for them, and re-layouts: 5.1 us -> 0.98 us  [fused(): w_second[:, :, i:i + last_width]]
    convert_element_type x1 -> x0, other arithmetic: 3.22 us -> none  [per_device(): mix = (numer_own / total_own[:, :, None]).astype(jnp.bfloat16)]
  transfers between devices with their start and end apart: 4 -> 0, of which waited for: 3 -> 0; matrix products, arithmetic and copies ran while one was open for 3% -> 0% of each run, Pallas kernels for 0% -> 0%
where the time goes in v2:
time: 197 us
  Pallas kernels  190 us (96%)
  local copies, waits for them, and re-layouts  4.29 us (2%)
  other arithmetic  2.78 us (1%)
    pallas_call x1, Pallas kernels, fused(): pl.pallas_call(functools.partial(fused_kernel, nb, tiles, deep_rows), out...  190 us

profile of v2, /device:TPU:0, one launch (start us, length us, event | category | flops | bytes accessed | tf_op | source)
XLA Modules:
  0.0 197.1 jit_solution(8471656404439277317)
XLA Ops:
  0.0 1.2 fusion.1
  1.3 0.4 copy.11
  1.7 1.1 pad.4.gate
  2.8 1.0 fusion.2
  3.7 1.6 pad_maximum_fusion.packed
  5.4 190.0 %shard_map.73 = f32[768,2]{1,0:T(8,128)} custom-call(bf16[768,3328]{1,0:T(8,128)(2,1)} %pooled.1, bf16[3328,128]{1,0:T(8,128)(2,1)} %pad.4.gate, bf16[4,208,1024]{2,1,0:T(8,128)(2,1)} %w_first.1, bf16[4,160,256]{2,1,0:T(8,128)(2,1)} %pad_maximum_fusion.packed, bf16[2,256,128]{2,1,0:T(8,128)(2,1)} %tower_hidden.1, bf16[2,128]{1,0:T(2,128)(2,1)} %tower_out.1), custom_call_target="tpu_custom_call" | custom-call | tf_op jit(solution)/shard_map/pallas_call | solution.py:336
  195.4 1.7 copy.12
  (2 shorter events, 0.1 us)

commit v3 on v2

--- a/solution.py
+++ b/solution.py
@@ -18,7 +18,7 @@
 
 def fused_kernel(
     nb, tiles, deep_rows,
-    pooled, gate, w_first, packed, tower_hidden, tower_out, out,
+    pooled, gate, w_first, w_second, w_third, tower_hidden, tower_out, out,
     buf, dbuf, first, outs, outs_rx, wts, wts_rx, acc,
     loc, recv, szp, szm, sy, ssib, brecv, bzp, bzm, by, bsib, xs, xr, ws, wr,
 ):
@@ -43,8 +43,21 @@
             buf.at[k, b], loc.at[k],
         )
 
-    deep_copy = pltpu.make_async_copy(packed, dbuf.at[b], loc.at[chunks])
-    deep_copy.start()
+    pieces = w_second.shape[2] // w_third.shape[2]
+    deep_copies = [
+        pltpu.make_async_copy(
+            w_second.at[:, :, pl.ds(h * w_third.shape[2], w_third.shape[2])],
+            dbuf.at[b, :, pl.ds(h * deep_rows, deep_rows)], loc.at[chunks + h],
+        )
+        for h in range(pieces)
+    ] + [
+        pltpu.make_async_copy(
+            w_third, dbuf.at[b, :, pl.ds(pieces * deep_rows, w_third.shape[1])],
+            loc.at[chunks + pieces],
+        )
+    ]
+    for copy in deep_copies:
+        copy.start()
 
     @pl.loop(0, chunks)
     def _(k):
@@ -129,7 +142,8 @@
         def _():
             bmove(slot, bzm.at[yy, zz], down).start()
 
-    deep_copy.wait()
+    for copy in deep_copies:
+        copy.wait()
     bmove(b, by.at[0], across).start()
     b_send_z(b, y, z)
     bmove(b, bsib.at[y, z], sib).start()
@@ -209,7 +223,6 @@
             width = dbuf.shape[3]
             low, high = first[0, rows, :], first[1, rows, :]
             total = None
-            pieces = (dbuf.shape[2] - 1) // deep_rows
             for h in range(pieces):
                 w2 = dbuf[:, e, pl.ds(h * deep_rows, deep_rows), :].reshape(-1, width)
                 second = dot(low, w2[:wide]) + dot(high, w2[wide:])
@@ -325,29 +338,26 @@
     gate = jnp.roll(gate_weight, -me * tasks, axis=2)
     gate = jnp.transpose(gate, (0, 2, 1)).reshape(width_in, all_tasks * experts)
     gate = jnp.pad(gate, ((0, 0), (0, 128 - all_tasks * experts)))
-    packed = jnp.concatenate(
-        [w_second[:, :, i : i + last_width] for i in range(0, deep_width, last_width)]
-        + [w_third],
-        axis=1,
-    )
+    pieces = deep_width // last_width
+    packed_rows = pieces * deep_rows + last_rows
     dma = pltpu.SemaphoreType.DMA
     vmem = pl.BlockSpec(memory_space=pltpu.VMEM)
     anywhere = pl.BlockSpec(memory_space=pl.ANY)
     return pl.pallas_call(
         functools.partial(fused_kernel, nb, tiles, deep_rows),
         out_shape=jax.ShapeDtypeStruct((tokens, tasks), F32),
-        in_specs=[vmem, vmem, anywhere, anywhere, vmem, vmem],
+        in_specs=[vmem, vmem, anywhere, anywhere, anywhere, vmem, vmem],
         out_specs=vmem,
         scratch_shapes=[
             pltpu.VMEM((chunks, nb, rows, wide), BF16),
-            pltpu.VMEM((nb,) + packed.shape, BF16),
+            pltpu.VMEM((nb, experts, packed_rows, last_width), BF16),
             pltpu.VMEM((2, tokens, wide), BF16),
             pltpu.VMEM((experts, tokens, last_width), BF16),
             pltpu.VMEM((experts, tokens, last_width), BF16),
             pltpu.VMEM((tokens, 128), F32),
             pltpu.VMEM((tokens, 128), F32),
             pltpu.VMEM((tasks, tokens, last_width), F32),
-            dma((chunks + 1,)),
+            dma((chunks + pieces + 1,)),
             dma((chunks, nb)),
             dma((chunks, nz)),
             dma((chunks, nz)),
@@ -366,7 +376,7 @@
         compiler_params=pltpu.CompilerParams(
             collective_id=0, has_side_effects=True, vmem_limit_bytes=VMEM_BYTES
         ),
-    )(pooled, gate, w_first, packed, tower_hidden, tower_out)
+    )(pooled, gate, w_first, w_second, w_third, tower_hidden, tower_out)
 
 
 def gathered_first(pooled, gate_weight, w_first, w_second, w_third, tower_hidden, tower_out):

time: 197 us -> 195 us (0.990)
  no operation moved by 1% of the time
where the time goes in v3:
time: 195 us
  Pallas kernels  190 us (97%)
  local copies, waits for them, and re-layouts  3.31 us (2%)
    pallas_call x1, Pallas kernels, fused(): pl.pallas_call(functools.partial(fused_kernel, nb, tiles, deep_rows), out...  190 us

profile of v3, /device:TPU:0, one launch (start us, length us, event | category | flops | bytes accessed | tf_op | source)
XLA Modules:
  0.0 194.6 jit_solution(17409748791912830792)
XLA Ops:
  0.0 1.2 fusion.1
  1.3 0.4 copy.11
  1.7 1.1 pad.4.gate
  2.8 190.0 %shard_map.73 = f32[768,2]{1,0:T(8,128)} custom-call(bf16[768,3328]{1,0:T(8,128)(2,1)} %pooled.1, bf16[3328,128]{1,0:T(8,128)(2,1)} %pad.4.gate, bf16[4,208,1024]{2,1,0:T(8,128)(2,1)} %w_first.1, bf16[4,64,512]{2,1,0:T(8,128)(2,1)} %w_second.1, bf16[4,32,256]{2,1,0:T(8,128)(2,1)} %w_third.1, bf16[2,256,128]{2,1,0:T(8,128)(2,1)} %tower_hidden.1, ...), custom_call_target="tpu_custom_call" | custom-call | tf_op jit(solution)/shard_map/pallas_call | solution.py:346
  192.8 1.7 copy.12
  (2 shorter events, 0.1 us)
